TPU v7x, 32 devices: a whole 2x2x4 slice. The times are simulated.
32 devices in a mesh: phi: 8 (over z, core), gz: 4 (over y, x).
Axes of the slice: x: 2, y: 2, z: 4, core: 2. Of those that a mesh axis runs over, the one named last changes fastest.
Arguments:
- charge: float32 [1024, 64, 256], P('phi', 'gz'), may hold values from -24 to 24
- outer_held: int32 [64], replicated, may hold values 0 or 1
- end_held: int32 [256], replicated, may hold values 0 or 1
Outputs:
- potential: float32 [1024, 64, 256], P('phi', 'gz')
- scales: float32 [2, 1024], P(None, 'phi')
Inputs may be any that keep to these rules, and one draw needn't show every extreme that they name: `outer_held`: 1 holds the boundary at zero potential, 0 leaves it without flux. `end_held`: 1 holds both z ends of the radial cell at zero potential, 0 leaves them without flux.
All inputs are finite; a program needn't handle non-finite values.
Results may differ from a plain program's by a relative error of at most 0.0003.
Values sent between devices are 32-bit elements; how exact they have to be, the bound alone decides.
No kernel may reach another device: no remote copies, remote signals or barrier semaphores. Data moves between devices by JAX's collectives and lax.ppermute only.
A program may use at most 128 MiB of HBM per device.

v0:
```python
import math

import jax
import jax.numpy as jnp
from jax import lax
from jax.sharding import PartitionSpec as P

NPHI = 1024
VCYC = 2
NU = 2
KC = 3
RIN = 131


relaxation = 0.8
small_floor = 1e-06


def hartley_table(length):
    row_ids = lax.broadcasted_iota(jnp.int32, (length, length), 0)
    col_ids = lax.broadcasted_iota(jnp.int32, (length, length), 1)
    phases = (row_ids * col_ids % length).astype(jnp.float32) * (2.0 * math.pi / length)
    return (jnp.cos(phases) + jnp.sin(phases)) * (1.0 / math.sqrt(length))


def transform_rows(hartley, values):
    flat = values.reshape(values.shape[0], -1)
    result = jnp.dot(
        hartley, flat, precision=lax.Precision.HIGHEST, preferred_element_type=jnp.float32
    )
    return result.reshape(values.shape)


def radial_terms(radial_count, coarse):
    position = jnp.arange(radial_count, dtype=jnp.float32)
    if coarse:
        radius = RIN + 2.0 * position + 1.0
        return (radius, (radius - 1.0) / (4.0 * radius), (radius + 1.0) / (4.0 * radius), 0.25)
    radius = RIN + position + 0.5
    return (radius, (radius - 0.5) / radius, (radius + 0.5) / radius, 1.0)


def diagonal(mode_ids, axial_ids, total_axial, radial, outer_bc, end_bc):
    radius, inward, outward, axial = radial
    last_radial = radius.shape[0] - 1
    radial_ids = jnp.arange(radius.shape[0], dtype=jnp.int32)
    open_out = (radial_ids[None, :] == last_radial) & (outer_bc[:, None] == 0)
    open_low = (axial_ids[:, None] == 0) & (end_bc[None, :] == 0)
    open_high = (axial_ids[:, None] == total_axial - 1) & (end_bc[None, :] == 0)
    baseline = inward[None, :] + outward[None, :] * jnp.where(open_out, 0.0, 1.0)
    baseline = baseline + axial * (jnp.where(open_low, 0.0, 1.0) + jnp.where(open_high, 0.0, 1.0))
    mode_order = jnp.minimum(mode_ids, NPHI - mode_ids).astype(jnp.float32)
    return (
        baseline[None] + (mode_order * mode_order)[:, None, None] / (radius * radius)[None, None, :]
    )


def neighbours(extended, radial):
    radius, inward, outward, axial = radial
    middle = extended[:, 1:-1, :]
    zero_edge = jnp.zeros_like(middle[:, :, :1])
    below_r = jnp.concatenate([zero_edge, middle[:, :, :-1]], axis=2)
    above_r = jnp.concatenate([middle[:, :, 1:], zero_edge], axis=2)
    return axial * (extended[:, 2:, :] + extended[:, :-2, :]) + inward * below_r + outward * above_r


def relax_step(extended, source, diag_part, radial):
    middle = extended[:, 1:-1, :]
    return (
        middle
        + relaxation * (source + neighbours(extended, radial) - diag_part * middle) / diag_part
    )


def operate(extended, diag_part, radial):
    return diag_part * extended[:, 1:-1, :] - neighbours(extended, radial)


def pad_axial(values):
    return jnp.pad(values, ((0, 0), (1, 1), (0, 0)))


def restrict(residual):
    modes, cells_z, cells_r = residual.shape
    return residual.reshape(modes, cells_z // 2, 2, cells_r // 2, 2).sum(axis=(2, 4)) * 0.25


def prolong(correction):
    return jnp.repeat(jnp.repeat(correction, 2, axis=1), 2, axis=2)


def body(charge, outer_held, end_held):
    hartley = hartley_table(NPHI)
    mode_count = charge.shape[0]
    cells_z = charge.shape[1]
    cells_r = charge.shape[2]
    total_z = cells_z * lax.axis_size("gz")
    spectrum_rows = transform_rows(
        hartley, lax.all_to_all(charge, "phi", split_axis=1, concat_axis=0, tiled=True)
    )
    spectrum = lax.all_to_all(spectrum_rows, "phi", split_axis=0, concat_axis=1, tiled=True)
    fine_terms = radial_terms(cells_r, False)
    coarse_terms = radial_terms(cells_r // 2, True)
    own = lax.all_to_all(spectrum, "gz", split_axis=0, concat_axis=1, tiled=True)
    few = own.shape[0]
    own_modes = (
        lax.axis_index("phi") * mode_count
        + lax.axis_index("gz") * few
        + jnp.arange(few, dtype=jnp.int32)
    )
    full_diag = diagonal(
        own_modes, jnp.arange(total_z, dtype=jnp.int32), total_z, fine_terms, outer_held, end_held
    )
    half_diag = diagonal(
        own_modes,
        jnp.arange(total_z // 2, dtype=jnp.int32),
        total_z // 2,
        coarse_terms,
        outer_held[0::2],
        end_held[0::2],
    )
    local_solution = jnp.zeros_like(own)
    local_rows = []
    for cycle_index in range(VCYC):
        for sweep_index in range(NU):
            local_solution = relax_step(pad_axial(local_solution), own, full_diag, fine_terms)
        residual = own - operate(pad_axial(local_solution), full_diag, fine_terms)
        coarse_rhs = restrict(residual)
        estimate = relaxation * coarse_rhs / half_diag
        for sweep_index in range(KC):
            estimate = relax_step(pad_axial(estimate), coarse_rhs, half_diag, coarse_terms)
        spread = prolong(estimate)
        image = operate(pad_axial(spread), full_diag, fine_terms)
        top = jnp.sum(residual * image, axis=(1, 2))
        bottom = jnp.sum(image * image, axis=(1, 2))
        factor = top / (bottom + small_floor)
        local_solution = local_solution + factor[:, None, None] * spread
        for sweep_index in range(NU):
            local_solution = relax_step(pad_axial(local_solution), own, full_diag, fine_terms)
        local_rows.append(factor)
    solution = lax.all_to_all(local_solution, "gz", split_axis=1, concat_axis=0, tiled=True)
    scales = lax.all_gather(jnp.stack(local_rows), "gz", axis=1, tiled=True)
    rows_back = transform_rows(
        hartley, lax.all_to_all(solution, "phi", split_axis=1, concat_axis=0, tiled=True)
    )
    potential = lax.all_to_all(rows_back, "phi", split_axis=0, concat_axis=1, tiled=True)
    return (potential, scales)


def solution(mesh):
    in_specs = (P("phi", "gz", None), P(), P())
    out_specs = (P("phi", "gz", None), P(None, "phi"))
    return jax.shard_map(body, mesh=mesh, in_specs=in_specs, out_specs=out_specs, check_vma=False)
```

profile of v0, /device:TPU:0, one launch (start us, length us, event | category | flops | bytes accessed | tf_op | source)
XLA Modules:
  0.0 458.6 jit_solution(12452107879361032873)
XLA Ops:
  0.6 2.8 copy.105
  3.4 55.2 %all_to_all.102 = f32[128,16,256]{2,0,1:T(8,128)S(1)} all-to-all(f32[128,16,256]{2,0,1:T(8,128)S(1)} %copy.105), channel_id=1, replica_groups=mesh['phi'=8,'gz'=4] {'phi'}, dimensions={1} | all-to-all | bytes 4194304 | tf_op jit(solution)/shard_map/all_to_all | solution.py:99
  58.6 1.8 copy.106
  60.4 2.1 copy.146
  62.5 24.6 %fusion.5 = f32[1024,2,256]{2,0,1:T(8,128)S(1)} fusion(f32[2,256,1024]{2,1,0:T(8,128)S(1)} %bitcast.91), kind=kOutput, calls=%fused_computation.28 | convolution fusion | flops 6459228160 | bytes 4194304 | tf_op jit(solution)/shard_map/dot_general | solution.py:28
  87.1 2.9 copy.107
  90.0 3.7 all-to-all-start.1
  93.9 48.8 %all-to-all-done.1 = f32[1024,2,256]{2,1,0:T(2,128)S(1)} async-done(((f32[1024,2,256]{2,1,0:T(2,128)}), f32[1024,2,256]{2,1,0:T(2,128)S(1)}, u32[]{:S(2)}, u32[]{:S(2)}) %all-to-all-start.1) | async-done | bytes 2097184 | tf_op jit(solution)/shard_map/all_to_all | solution.py:101
  143.0 2.5 copy.110
  145.6 3.8 all-to-all-start.2
  150.2 23.9 %all-to-all-done.2 = f32[128,16,256]{2,1,0:T(8,128)S(1)} async-done(((f32[128,16,256]{2,1,0:T(8,128)}), f32[128,16,256]{2,1,0:T(8,128)S(1)}, u32[]{:S(2)}, u32[]{:S(2)}) %all-to-all-start.2) | async-done | bytes 2097184 | tf_op jit(solution)/shard_map/all_to_all | solution.py:104
  174.2 1.3 copy-done.8
  175.5 1.8 copy.111
  177.9 0.7 fusion.156
  178.6 1.5 fusion.72
  180.1 0.7 fusion.155
  181.4 2.8 fusion.20
  184.2 6.3 %copy.112 = f32[32,64,256]{0,2,1:T(8,128)} copy(f32[32,64,256]{2,1,0:T(8,128)} %fusion.20) | data formatting | bytes 4194304 | tf_op jit(solution)/shard_map/sub | solution.py:127
  190.6 10.8 %reduce_sum.54 = f32[32,32,128]{0,2,1:T(8,128)} reduce(f32[32,32,2,128,2]{0,4,3,2,1:T(2,128)} %bitcast.76, f32[]{:T(128)} %constant.34.clone.1), dimensions={2,4}, to_apply=%region_0.1 | reduce | flops 393216 | bytes 2621444 | tf_op jit(solution)/shard_map/reduce_sum | solution.py:85
  201.4 2.3 copy.113
  206.0 1.1 broadcast_in_dim.39
  207.1 4.1 copy.116
  211.2 4.1 broadcast_in_dim.40
  215.3 5.0 %copy.117 = f32[32,64,256]{2,1,0:T(8,128)} copy(f32[32,64,256]{1,0,2:T(8,128)} %bitcast.77) | data formatting | bytes 4194304 | tf_op jit(solution)/shard_map/reshape | solution.py:89
  220.3 3.2 fusion.154
  223.8 2.0 multiply_reduce_fusion.2
  226.1 0.7 fusion.153
  226.9 1.5 fusion.73
  228.3 0.7 fusion.152
  229.1 1.5 fusion.74
  230.6 0.7 fusion.151
  231.3 1.5 fusion.75
  232.8 0.7 fusion.150
  233.6 1.5 fusion.76
  235.1 0.9 fusion.149
  236.4 2.8 fusion.53
  239.2 6.3 %copy.122 = f32[32,64,256]{0,2,1:T(8,128)} copy(f32[32,64,256]{2,1,0:T(8,128)} %fusion.53) | data formatting | bytes 4194304 | tf_op jit(solution)/shard_map/sub | solution.py:127
  245.5 10.8 %reduce_sum.57 = f32[32,32,128]{0,2,1:T(8,128)} reduce(f32[32,32,2,128,2]{0,4,3,2,1:T(2,128)} %bitcast.75, f32[]{:T(128)} %constant.34.clone.1), dimensions={2,4}, to_apply=%region_3.4 | reduce | flops 393216 | bytes 2621444 | tf_op jit(solution)/shard_map/reduce_sum | solution.py:85
  256.3 2.3 copy.123
  261.0 1.1 broadcast_in_dim.41
  262.1 4.1 copy.126
  266.1 4.1 broadcast_in_dim.42
  270.3 4.8 %copy.127 = f32[32,64,256]{2,1,0:T(8,128)} copy(f32[32,64,256]{1,0,2:T(8,128)} %bitcast.78) | data formatting | bytes 4194304 | tf_op jit(solution)/shard_map/reshape | solution.py:89
  275.1 3.2 fusion.148
  278.6 2.0 multiply_reduce_fusion
  280.9 0.7 fusion.147
  281.6 1.5 fusion.77
  283.1 0.7 fusion.146
  283.8 1.5 fusion.78
  285.3 1.2 copy.132
  286.5 27.4 %all_to_all.103 = f32[32,64,256]{2,0,1:T(8,128)S(1)} all-to-all(f32[32,64,256]{2,0,1:T(8,128)S(1)} %copy.132), channel_id=1, replica_groups=mesh['phi'=8,'gz'=4] {'gz'}, dimensions={1} | all-to-all | bytes 4194304 | tf_op jit(solution)/shard_map/all_to_all | solution.py:141
  313.9 1.2 copy.134
  315.1 1.2 copy.135
  316.3 51.9 %all_to_all.104 = f32[128,16,256]{2,0,1:T(8,128)S(1)} all-to-all(f32[128,16,256]{2,0,1:T(8,128)S(1)} %copy.135), channel_id=1, replica_groups=mesh['phi'=8,'gz'=4] {'phi'}, dimensions={1} | all-to-all | bytes 4194304 | tf_op jit(solution)/shard_map/all_to_all | solution.py:144
  368.3 1.8 copy.136
  370.1 2.1 copy.145
  372.2 24.6 %fusion.3 = f32[1024,2,256]{2,0,1:T(8,128)S(1)} fusion(f32[2,256,1024]{2,1,0:T(8,128)S(1)} %bitcast.92), kind=kOutput, calls=%fused_computation.26 | convolution fusion | flops 6459228160 | bytes 4194304 | tf_op jit(solution)/shard_map/dot_general | solution.py:28
  396.8 2.9 copy.137
  399.7 3.6 all-to-all-start.5
  403.3 7.5 %all-gather = f32[4,32,2]{1,2,0:T(2,128)S(1)} all-gather(f32[1,32,2]{1,2,0:T(2,128)S(1)} %maximum_bitcast_fusion), channel_id=1, replica_groups=mesh['phi'=8,'gz'=4] {'gz'}, dimensions={0}, use_global_device_ids=true | all-gather | bytes 1280 | tf_op jit(solution)/shard_map/all_gather | solution.py:142
  410.8 0.6 reshape.477
  411.5 40.8 %all-to-all-done.5 = f32[1024,2,256]{2,1,0:T(2,128)S(1)} async-done(((f32[1024,2,256]{2,1,0:T(2,128)}), f32[1024,2,256]{2,1,0:T(2,128)S(1)}, u32[]{:S(2)}, u32[]{:S(2)}) %all-to-all-start.5) | async-done | bytes 2097184 | tf_op jit(solution)/shard_map/all_to_all | solution.py:146
  452.3 2.5 copy.138
  454.8 3.6 all_to_all.95
  (67 shorter events, 8.4 us)
Async XLA Ops:
  90.0 3.9 copy-start.10
  90.0 52.7 %all-to-all-start.1 = ((f32[1024,2,256]{2,1,0:T(2,128)}), f32[1024,2,256]{2,1,0:T(2,128)S(1)}, u32[]{:S(2)}, u32[]{:S(2)}) async-start(f32[1024,2,256]{2,1,0:T(2,128)} %copy.107), calls=%async_computation.1 | async-start | bytes 4194304 | tf_op jit(solution)/shard_map/all_to_all | solution.py:101
  145.6 4.1 copy-start.9
  145.6 28.6 %all-to-all-start.2 = ((f32[128,16,256]{2,1,0:T(8,128)}), f32[128,16,256]{2,1,0:T(8,128)S(1)}, u32[]{:S(2)}, u32[]{:S(2)}) async-start(f32[128,16,256]{2,1,0:T(8,128)} %copy.110), calls=%async_computation.2 | async-start | bytes 4194304 | tf_op jit(solution)/shard_map/all_to_all | solution.py:104
  174.2 1.3 copy-start.8
  180.1 1.3 copy-start.4
  220.3 3.2 copy-start
  220.3 3.5 copy-start.7
  223.8 2.0 copy-start.5
  235.1 1.3 copy-start.2
  275.1 3.2 copy-start.1
  275.1 3.5 copy-start.6
  278.5 2.0 copy-start.3
  399.7 52.6 %all-to-all-start.5 = ((f32[1024,2,256]{2,1,0:T(2,128)}), f32[1024,2,256]{2,1,0:T(2,128)S(1)}, u32[]{:S(2)}, u32[]{:S(2)}) async-start(f32[1024,2,256]{2,1,0:T(2,128)} %copy.137), calls=%async_computation.5 | async-start | bytes 4194304 | tf_op jit(solution)/shard_map/all_to_all | solution.py:146
where the time goes:
time: 462 us; the launch traced here: 459 us
  blocking collectives  142 us (31%)
  waiting for transfers between devices  114 us (25%)
  local copies, waits for them, and re-layouts  95.5 us (21%)
  matrix products  49.2 us (11%)
  other arithmetic  45.9 us (10%)
  starting transfers between devices  11.2 us (2%)
    all_to_all x1, blocking collectives, body(): lax.all_to_all(charge, 'phi', split_axis=1, concat_axis=0, tiled=True)  55.2 us
    all_to_all x1, blocking collectives, body(): lax.all_to_all(solution, 'phi', split_axis=1, concat_axis=0, tiled=True)  51.9 us
    dot_general x2, matrix products, transform_rows(): jnp.dot(hartley, flat, precision=lax.Precision.HIGHEST, preferred_element...  49.2 us
    all_to_all x1, waiting for transfers between devices, body(): lax.all_to_all(spectrum_rows, 'phi', split_axis=0, concat_axis=1, tiled=T...  48.8 us
    all_to_all x1, waiting for transfers between devices, body(): lax.all_to_all(rows_back, 'phi', split_axis=0, concat_axis=1, tiled=True)  40.8 us
    all_to_all x1, blocking collectives, body(): lax.all_to_all(local_solution, 'gz', split_axis=1, concat_axis=0, tiled=T...  27.4 us
    all_to_all x1, waiting for transfers between devices, body(): lax.all_to_all(spectrum, 'gz', split_axis=0, concat_axis=1, tiled=True)  23.9 us
    reduce_sum x2, other arithmetic, restrict(): residual.reshape(modes, cells_z // 2, 2, cells_r // 2, 2).sum(axis=(2, 4))  21.6 us
  transfers between devices with their start and end apart: 3, of which 3 were waited for; matrix products, arithmetic and copies ran while one was open for 0% of the time, Pallas kernels for 0%

commit v1 on v0

v1 whole, which is shorter than its diff:
```python
import functools
import math

import jax
import jax.numpy as jnp
import numpy as np
from jax import lax
from jax.experimental import pallas as pl
from jax.experimental.pallas import tpu as pltpu
from jax.sharding import PartitionSpec as P

VCYC = 2
NU = 2
KC = 3
RIN = 131

relaxation = 0.8
small_floor = 1e-06

VMEM_LIMIT = 60 * 1024 * 1024


def split_bf16(values):
    high = values.astype(jnp.bfloat16)
    low = (values - high.astype(jnp.float32)).astype(jnp.bfloat16)
    return high, low


def hartley_halves(length):
    half = length // 2
    modes = np.arange(half)[:, None]
    cells = np.arange(half)[None, :]
    tables = []
    for parity in range(2):
        phases = ((2 * modes + parity) * cells % length) * (2.0 * math.pi / length)
        tables.append((np.cos(phases) + np.sin(phases)) / math.sqrt(length))
    exact = np.stack(tables)
    high = exact.astype(jnp.bfloat16)
    low = (exact - high.astype(np.float64)).astype(jnp.bfloat16)
    return np.stack([high, low], axis=1)


def parity_order(cells):
    order = np.concatenate([np.arange(0, cells, 2), np.arange(1, cells, 2)])
    matrix = np.zeros((cells, cells), np.float32)
    matrix[order, np.arange(cells)] = 1.0
    return matrix.astype(jnp.bfloat16)


def dot32(left, right):
    return jnp.dot(left, right, preferred_element_type=jnp.float32)


def three_dots(table_high, table_low, high, low):
    return dot32(table_high, high) + (dot32(table_high, low) + dot32(table_low, high))


def permuted_split(values, order):
    high, low = split_bf16(values)
    return dot32(high, order).astype(jnp.bfloat16), dot32(low, order).astype(jnp.bfloat16)


def forward_kernel(cells_ref, table_ref, order_ref, out_ref):
    sources, _, rows, cells_r = cells_ref.shape
    whole = cells_ref[...].reshape(sources * rows, cells_r)
    half = whole.shape[0] // 2
    for parity in range(2):
        mixed = whole[:half] + whole[half:] if parity == 0 else whole[:half] - whole[half:]
        high, low = permuted_split(mixed, order_ref[...])
        out_ref[0, parity] = three_dots(table_ref[parity, 0], table_ref[parity, 1], high, low)


def forward_transform(cells, tables, order):
    sources, rows_z, rows, cells_r = cells.shape
    half = sources * rows // 2
    return pl.pallas_call(
        forward_kernel,
        grid=(rows_z,),
        in_specs=[
            pl.BlockSpec((sources, 1, rows, cells_r), lambda z: (0, z, 0, 0)),
            pl.BlockSpec(tables.shape, lambda z: (0, 0, 0, 0)),
            pl.BlockSpec(order.shape, lambda z: (0, 0)),
        ],
        out_specs=pl.BlockSpec((1, 2, half, cells_r), lambda z: (z, 0, 0, 0)),
        out_shape=jax.ShapeDtypeStruct((rows_z, 2, half, cells_r), jnp.float32),
        compiler_params=pltpu.CompilerParams(vmem_limit_bytes=VMEM_LIMIT),
        name="forward_transform",
    )(cells, tables, order)


def backward_kernel(modes_ref, table_ref, order_ref, out_ref):
    dests, _, rows, cells_r = out_ref.shape
    half = dests * rows // 2
    parts = []
    for parity in range(2):
        high, low = permuted_split(modes_ref[0, parity], order_ref[...])
        parts.append(three_dots(table_ref[parity, 0], table_ref[parity, 1], high, low))
    out_ref[: dests // 2, 0] = (parts[0] + parts[1]).reshape(dests // 2, rows, cells_r)
    out_ref[dests // 2 :, 0] = (parts[0] - parts[1]).reshape(dests // 2, rows, cells_r)


def backward_transform(modes, tables, order, dests):
    rows_z, _, half, cells_r = modes.shape
    rows = 2 * half // dests
    return pl.pallas_call(
        backward_kernel,
        grid=(rows_z,),
        in_specs=[
            pl.BlockSpec((1, 2, half, cells_r), lambda z: (z, 0, 0, 0)),
            pl.BlockSpec(tables.shape, lambda z: (0, 0, 0, 0)),
            pl.BlockSpec(order.shape, lambda z: (0, 0)),
        ],
        out_specs=pl.BlockSpec((dests, 1, rows, cells_r), lambda z: (0, z, 0, 0)),
        out_shape=jax.ShapeDtypeStruct((dests, rows_z, rows, cells_r), jnp.float32),
        compiler_params=pltpu.CompilerParams(vmem_limit_bytes=VMEM_LIMIT),
        name="backward_transform",
    )(modes, tables, order)


def block_of(count, most):
    block = most
    while count % block:
        block //= 2
    return block


def solve_kernel(outer_ref, source_ref, order2_ref, ends_ref, out_ref, scale_ref,
                 ping, pong, rest, fine_w, fine_d, fine_g, rhs, thin, thick, coarse_w):
    total_z, modes, cells_r = source_ref.shape
    lanes = cells_r // 2
    total_y = total_z // 2
    tile = min(8, modes)
    tiles = modes // tile
    block_z = block_of(total_z, 8)
    block_y = block_of(total_y, 4)

    spot = lax.broadcasted_iota(jnp.int32, (1, lanes), 1)
    position = spot.astype(jnp.float32)
    first = spot == 0
    last = spot == lanes - 1
    fine = []
    for parity in range(2):
        radius = RIN + (2.0 * position + parity) + 0.5
        fine.append((radius, (radius - 0.5) / radius, (radius + 0.5) / radius))
    coarse_radius = RIN + 2.0 * position + 1.0
    coarse_in = (coarse_radius - 1.0) / (4.0 * coarse_radius)
    coarse_out = (coarse_radius + 1.0) / (4.0 * coarse_radius)
    in_even = jnp.where(first, 0.0, fine[0][1])
    out_even = fine[0][2]
    in_odd = fine[1][1]
    out_odd = jnp.where(last, 0.0, fine[1][2])
    coarse_below = jnp.where(first, 0.0, coarse_in)
    coarse_above = jnp.where(last, 0.0, coarse_out)

    order2 = order2_ref[...]
    for held in range(2):
        for end in range(2):
            variant = held + 2 * end
            for parity in range(2):
                radius, inward, outward = fine[parity]
                open_ends = jnp.where(ends_ref[:, parity * lanes:(parity + 1) * lanes] == 0, 1.0, 0.0)
                base = inward + outward
                if held == 0 and parity == 1:
                    base = inward + jnp.where(last, 0.0, outward)
                base = base + 2.0
                if end:
                    base = base - (2.0 * open_ends if total_z == 1 else open_ends)
                full = base + order2 / (radius * radius)
                there = slice(parity * lanes, (parity + 1) * lanes)
                fine_d[variant, :, there] = full
                fine_w[variant, :, there] = relaxation / full
                fine_g[variant, :, there] = full - 1.0 - (fine[0][2] if parity == 0 else fine[1][1])
            open_ends = jnp.where(ends_ref[:, :lanes] == 0, 0.25, 0.0)
            base = coarse_in + (jnp.where(last, 0.0, coarse_out) if held == 0 else coarse_out)
            base = base + 0.5
            if end:
                base = base - (2.0 * open_ends if total_y == 1 else open_ends)
            coarse_w[variant] = relaxation / (base + order2 / (coarse_radius * coarse_radius))

    zero_fine = jnp.zeros((1, modes, cells_r), jnp.float32)
    zero_coarse = jnp.zeros((1, modes, lanes), jnp.float32)
    for buffer in (ping, pong):
        buffer[pl.ds(0, 1)] = zero_fine
        buffer[pl.ds(total_z + 1, 1)] = zero_fine
    for buffer in (rhs, thin, thick):
        buffer[pl.ds(0, 1)] = zero_coarse
        buffer[pl.ds(total_y + 1, 1)] = zero_coarse

    def fine_variant(z):
        ends = jnp.where((z == 0) | (z == total_z - 1), 2, 0)
        return outer_ref[z] + ends

    def coarse_variant(y):
        ends = jnp.where((y == 0) | (y == total_y - 1), 2, 0)
        return outer_ref[2 * y] + ends

    even = pl.ds(0, lanes)
    odd = pl.ds(lanes, lanes)

    def each_fine(body):
        for step in range(tiles):
            there = pl.ds(step * tile, tile)

            def one(block, carry, there=there):
                body(block * block_z, there)
                return carry

            lax.fori_loop(0, total_z // block_z, one, 0)

    def each_coarse(body):
        for step in range(tiles):
            there = pl.ds(step * tile, tile)

            def one(block, carry, there=there):
                body(block * block_y, there)
                return carry

            lax.fori_loop(0, total_y // block_y, one, 0)

    def neighbour_sum(rows, at):
        before_e, before_o = rows[at - 1]
        here_e, here_o = rows[at]
        after_e, after_o = rows[at + 1]
        sum_e = (before_e + after_e) + (in_even * pltpu.roll(here_o, 1, 1) + out_even * here_o)
        sum_o = (before_o + after_o) + (in_odd * here_e + out_odd * pltpu.roll(here_e, lanes - 1, 1))
        return sum_e, sum_o

    def relax_rows(rows, z0, there, store):
        for at in range(block_z):
            z = z0 + at
            variant = fine_variant(z)
            sum_e, sum_o = neighbour_sum(rows, at + 1)
            here_e, here_o = rows[at + 1]
            new_e = (1.0 - relaxation) * here_e + fine_w[variant, there, even] * (source_ref[z, there, even] + sum_e)
            new_o = (1.0 - relaxation) * here_o + fine_w[variant, there, odd] * (source_ref[z, there, odd] + sum_o)
            store(z, there, new_e, new_o)

    def store_padded(buffer):
        def store(z, there, new_e, new_o):
            buffer[z + 1, there, even] = new_e
            buffer[z + 1, there, odd] = new_o
        return store

    def store_out(z, there, new_e, new_o):
        out_ref[z, there, even] = new_e
        out_ref[z, there, odd] = new_o

    def padded_rows(buffer, z0, there):
        return [(buffer[z0 + at, there, even], buffer[z0 + at, there, odd]) for at in range(block_z + 2)]

    def sweep(buffer, store):
        def body(z0, there):
            relax_rows(padded_rows(buffer, z0, there), z0, there, store)
        each_fine(body)

    def first_sweeps(store):
        def body(z0, there):
            rows = []
            for at in range(-1, block_z + 1):
                z = jnp.clip(z0 + at, 0, total_z - 1)
                variant = fine_variant(z)
                row_e = fine_w[variant, there, even] * source_ref[z, there, even]
                row_o = fine_w[variant, there, odd] * source_ref[z, there, odd]
                if at in (-1, block_z):
                    inside = jnp.where((z0 + at >= 0) & (z0 + at < total_z), 1.0, 0.0)
                    row_e = row_e * inside
                    row_o = row_o * inside
                rows.append((row_e, row_o))
            relax_rows(rows, z0, there, store)
        each_fine(body)

    def residual_pass(buffer):
        def body(z0, there):
            rows = padded_rows(buffer, z0, there)
            pair = None
            for at in range(block_z):
                z = z0 + at
                variant = fine_variant(z)
                sum_e, sum_o = neighbour_sum(rows, at + 1)
                here_e, here_o = rows[at + 1]
                left_e = (source_ref[z, there, even] + sum_e) - fine_d[variant, there, even] * here_e
                left_o = (source_ref[z, there, odd] + sum_o) - fine_d[variant, there, odd] * here_o
                rest[z, there, even] = left_e
                rest[z, there, odd] = left_o
                if at % 2 == 0:
                    pair = left_e + left_o
                else:
                    rhs[z0 // 2 + at // 2 + 1, there] = 0.25 * (pair + (left_e + left_o))
        each_fine(body)

    def coarse_rows(load, y0, there):
        return [load(y0 + at, there) for at in range(block_y + 2)]

    def coarse_relax(load, target):
        def body(y0, there):
            rows = coarse_rows(load, y0, there)
            for at in range(block_y):
                y = y0 + at
                here = rows[at + 1]
                total = 0.25 * (rows[at] + rows[at + 2]) + (
                    coarse_below * pltpu.roll(here, 1, 1) + coarse_above * pltpu.roll(here, lanes - 1, 1))
                weight = coarse_w[coarse_variant(y), there]
                target[y + 1, there] = (1.0 - relaxation) * here + weight * (rhs[y + 1, there] + total)
        each_coarse(body)

    def load_of(buffer):
        return lambda y, there: buffer[y, there]

    def load_first(y, there):
        inner = jnp.clip(y - 1, 0, total_y - 1)
        return coarse_w[coarse_variant(inner), there] * rhs[y, there]

    def coarse_solve():
        buffers = (thin, thick)
        load = load_first
        for step in range(KC):
            target = buffers[step % 2]
            coarse_relax(load, target)
            load = load_of(target)
        return buffers[(KC - 1) % 2]

    def image_scale(estimate, there):
        def one(block, carry):
            top, bottom = carry
            y0 = block * block_y
            rows = coarse_rows(load_of(estimate), y0, there)
            for at in range(block_y):
                here = rows[at + 1]
                side_e = in_even * pltpu.roll(here, 1, 1)
                side_o = out_odd * pltpu.roll(here, lanes - 1, 1)
                for low in range(2):
                    z = 2 * (y0 + at) + low
                    variant = fine_variant(z)
                    across = rows[at + 2 * low]
                    image_e = fine_g[variant, there, even] * here - (side_e + across)
                    image_o = fine_g[variant, there, odd] * here - (side_o + across)
                    top = top + (rest[z, there, even] * image_e + rest[z, there, odd] * image_o)
                    bottom = bottom + (image_e * image_e + image_o * image_o)
            return top, bottom

        nothing = jnp.zeros((tile, lanes), jnp.float32)
        top, bottom = lax.fori_loop(0, total_y // block_y, one, (nothing, nothing))
        top = jnp.sum(top, axis=1, keepdims=True)
        bottom = jnp.sum(bottom, axis=1, keepdims=True)
        return jnp.broadcast_to(top / (bottom + small_floor), (tile, lanes))

    def corrected_sweep(buffer, estimate, cycle, store):
        for step in range(tiles):
            there = pl.ds(step * tile, tile)
            scale = image_scale(estimate, there)
            scale_ref[cycle, there] = scale

            def one(block, carry, there=there, scale=scale):
                z0 = block * block_z
                rows = padded_rows(buffer, z0, there)
                added = []
                for at in range(-1, block_z // 2 + 1):
                    added.append(scale * estimate[z0 // 2 + at + 1, there])
                moved = []
                for at in range(block_z + 2):
                    plus = added[(at + 1) // 2]
                    moved.append((rows[at][0] + plus, rows[at][1] + plus))
                relax_rows(moved, z0, there, store)
                return carry

            lax.fori_loop(0, total_z // block_z, one, 0)

    for cycle in range(VCYC):
        if cycle == 0:
            first_sweeps(store_padded(ping))
            left = NU - 2
        else:
            left = NU
        here, other = ping, pong
        for _ in range(left):
            sweep(here, store_padded(other))
            here, other = other, here
        residual_pass(here)
        estimate = coarse_solve()
        for step in range(NU):
            final = cycle == VCYC - 1 and step == NU - 1
            store = store_out if final else store_padded(other)
            if step == 0:
                corrected_sweep(here, estimate, cycle, store)
            else:
                sweep(here, store)
            here, other = other, here
        ping, pong = here, other


def solve_modes(source, order2, outer_held, ends):
    total_z, modes, cells_r = source.shape
    lanes = cells_r // 2
    f32 = jnp.float32
    whole = pl.BlockSpec(memory_space=pltpu.VMEM)
    return pl.pallas_call(
        solve_kernel,
        in_specs=[pl.BlockSpec(memory_space=pltpu.SMEM), whole, whole, whole],
        out_specs=[whole, whole],
        out_shape=[
            jax.ShapeDtypeStruct((total_z, modes, cells_r), f32),
            jax.ShapeDtypeStruct((VCYC, modes, lanes), f32),
        ],
        scratch_shapes=[
            pltpu.VMEM((total_z + 2, modes, cells_r), f32),
            pltpu.VMEM((total_z + 2, modes, cells_r), f32),
            pltpu.VMEM((total_z, modes, cells_r), f32),
            pltpu.VMEM((4, modes, cells_r), f32),
            pltpu.VMEM((4, modes, cells_r), f32),
            pltpu.VMEM((4, modes, cells_r), f32),
            pltpu.VMEM((total_z // 2 + 2, modes, lanes), f32),
            pltpu.VMEM((total_z // 2 + 2, modes, lanes), f32),
            pltpu.VMEM((total_z // 2 + 2, modes, lanes), f32),
            pltpu.VMEM((4, modes, lanes), f32),
        ],
        compiler_params=pltpu.CompilerParams(vmem_limit_bytes=VMEM_LIMIT),
        name="solve_modes",
    )(outer_held, source, order2, ends)


def body(charge, outer_held, end_held):
    phi_size = lax.axis_size("phi")
    gz_size = lax.axis_size("gz")
    devices = phi_size * gz_size
    rows, cells_z, cells_r = charge.shape
    length = rows * phi_size
    rows_z = cells_z // phi_size
    total_z = cells_z * gz_size
    few = length // devices

    exact = hartley_halves(length)
    forward = jnp.asarray(exact)
    backward = lax.optimization_barrier(forward)
    backward = jnp.stack([backward[0], jnp.swapaxes(backward[1], 1, 2)])
    order = jnp.asarray(parity_order(cells_r))
    disorder = jnp.asarray(parity_order(cells_r).T)

    blocks = jnp.transpose(charge, (1, 0, 2)).reshape(phi_size, rows_z, rows, cells_r)
    blocks = lax.all_to_all(blocks, "phi", split_axis=0, concat_axis=0, tiled=True)
    modes = forward_transform(blocks, forward, order)

    modes = modes.reshape(rows_z, 2, phi_size, gz_size, few // 2, cells_r)
    modes = jnp.transpose(modes, (3, 2, 0, 1, 4, 5)).reshape(devices, rows_z, few, cells_r)
    own = lax.all_to_all(modes, ("gz", "phi"), split_axis=0, concat_axis=0, tiled=True)
    own = own.reshape(total_z, few, cells_r)

    place = lax.axis_index("phi") * gz_size + lax.axis_index("gz")
    slots = jnp.arange(few, dtype=jnp.int32)
    own_modes = place * few + 2 * (slots % (few // 2)) + slots // (few // 2)
    mode_order = jnp.minimum(own_modes, length - own_modes).astype(jnp.float32)
    order2 = (mode_order * mode_order)[:, None]
    ends = jnp.concatenate([end_held[0::2], end_held[1::2]])[None, :]
    solved, scale_lanes = solve_modes(own, order2, outer_held, ends)

    natural = scale_lanes[:, :, 0].reshape(VCYC, 2, few // 2)
    natural = jnp.transpose(natural, (0, 2, 1)).reshape(VCYC, few)
    scales = lax.all_gather(natural, "gz", axis=1, tiled=True)

    back = solved.reshape(devices, rows_z, few, cells_r)
    back = lax.all_to_all(back, ("gz", "phi"), split_axis=0, concat_axis=0, tiled=True)
    back = back.reshape(gz_size, phi_size, rows_z, 2, few // 2, cells_r)
    back = jnp.transpose(back, (2, 3, 1, 0, 4, 5)).reshape(rows_z, 2, length // 2, cells_r)
    cells = backward_transform(back, backward, disorder, phi_size)
    cells = lax.all_to_all(cells, "phi", split_axis=0, concat_axis=0, tiled=True)
    potential = jnp.transpose(cells.reshape(cells_z, rows, cells_r), (1, 0, 2))
    return (potential, scales)


def solution(mesh):
    in_specs = (P("phi", "gz", None), P(), P())
    out_specs = (P("phi", "gz", None), P(None, "phi"))
    return jax.shard_map(body, mesh=mesh, in_specs=in_specs, out_specs=out_specs, check_vma=False)
```

time: 462 us -> 291 us (0.63)
  blocking collectives: 142 us -> 62.4 us
  local copies, waits for them, and re-layouts: 95.5 us -> 16.9 us
  Pallas kernels: 0 us -> 63.6 us
  matrix products: 49.2 us -> 0 us
  other arithmetic: 45.9 us -> 4.22 us
  waiting for transfers between devices: 114 us -> 132 us
    all_to_all x3 -> x1, blocking collectives: 134 us -> 55.3 us  [body(): lax.all_to_all(blocks, 'phi', split_axis=0, concat_axis=0, tiled=True)]
    pallas_call x0 -> x3, Pallas kernels: none -> 63.6 us  [the longest x1 52.7 us: solve_modes(): pl.pallas_call(solve_kernel, in_specs=[pl.BlockSpec(memory_space=pltpu.SM...]
    dot_general x2 -> x0, matrix products: 49.2 us -> none  [transform_rows(): jnp.dot(hartley, flat, precision=lax.Precision.HIGHEST, preferred_element...]
    reduce_sum x4 -> x0, other arithmetic: 25.6 us -> none  [the longest x2 21.6 us: restrict(): residual.reshape(modes, cells_z // 2, 2, cells_r // 2, 2).sum(axis=(2, 4))]
    all_to_all x3, waiting for transfers between devices: 114 us -> 132 us  [the longest x1 48.4 us: body(): lax.all_to_all(modes, ('gz', 'phi'), split_axis=0, concat_axis=0, tiled=T...]
    all_to_all x10 -> x0, local copies, waits for them, and re-layouts: 16.9 us -> none  [the longest x2 6.18 us: body(): lax.all_to_all(rows_back, 'phi', split_axis=0, concat_axis=1, tiled=True)]
    reshape x4 -> x2, local copies, waits for them, and re-layouts: 17.9 us -> 2.63 us  [the longest x1 2.54 us: body(): potential = jnp.transpose(cells.reshape(cells_z, rows, cells_r), (1, 0, 2))]
    add x18 -> x0, other arithmetic: 13.8 us -> none  [the longest x13 13 us: relax_step(): middle + relaxation * (source + neighbours(extended, radial) - diag_part...]
  transfers between devices with their start and end apart: 3 -> 3, of which waited for: 3 -> 3; matrix products, arithmetic and copies ran while one was open for 0% -> 3% of each run, Pallas kernels for 0% -> 0%
where the time goes in v1:
time: 291 us; the launch traced here: 290 us
  waiting for transfers between devices  132 us (45%)
  Pallas kernels  63.6 us (22%)
  blocking collectives  62.4 us (21%)
  local copies, waits for them, and re-layouts  16.9 us (6%)
  starting transfers between devices  9.99 us (3%)
  other arithmetic  4.22 us (1%)
    all_to_all x1, blocking collectives, body(): lax.all_to_all(blocks, 'phi', split_axis=0, concat_axis=0, tiled=True)  55.3 us
    pallas_call x1, Pallas kernels, solve_modes(): pl.pallas_call(solve_kernel, in_specs=[pl.BlockSpec(memory_space=pltpu.SM...  52.7 us
    all_to_all x1, waiting for transfers between devices, body(): lax.all_to_all(modes, ('gz', 'phi'), split_axis=0, concat_axis=0, tiled=T...  48.4 us
    all_to_all x1, waiting for transfers between devices, body(): lax.all_to_all(back, ('gz', 'phi'), split_axis=0, concat_axis=0, tiled=True)  43 us
    all_to_all x1, waiting for transfers between devices, body(): lax.all_to_all(cells, 'phi', split_axis=0, concat_axis=0, tiled=True)  40.8 us
    all_gather x1, blocking collectives, body(): scales = lax.all_gather(natural, 'gz', axis=1, tiled=True)  7.1 us
  transfers between devices with their start and end apart: 3, of which 3 were waited for; matrix products, arithmetic and copies ran while one was open for 3% of the time, Pallas kernels for 0%

profile of v1, /device:TPU:0, one launch (start us, length us, event | category | flops | bytes accessed | tf_op | source)
XLA Modules:
  0.0 289.9 jit_solution(7459518278434522851)
XLA Ops:
  0.6 2.8 copy.30
  3.4 55.3 %all_to_all.20.cells_ref = f32[8,2,128,256]{3,2,1,0:T(8,128)} all-to-all(f32[8,2,128,256]{3,2,1,0:T(8,128)S(1)} %bitcast.36), channel_id=1, replica_groups=mesh['phi'=8,'gz'=4] {'phi'}, dimensions={0} | all-to-all | bytes 4194304 | tf_op jit(solution)/shard_map/all_to_all | solution.py:439
  58.7 5.4 %forward_transform.1 = f32[2,2,512,256]{3,2,1,0:T(8,128)} custom-call(f32[8,2,128,256]{3,2,1,0:T(8,128)} %all_to_all.20.cells_ref, bf16[2,2,512,512]{3,2,1,0:T(8,128)(2,1)} %constant.56.table_ref, bf16[256,256]{1,0:T(8,128)(2,1)} %constant.54.clone.order_ref), custom_call_target="tpu_custom_call" | custom-call | tf_op jit(solution)/shard_map/forward_transform/pallas_call | solution.py:76
  64.2 3.2 %copy.32 = f32[4,8,2,2,16,256]{5,4,3,2,1,0:T(8,128)} copy(f32[4,8,2,2,16,256]{5,4,0,1,3,2:T(8,128)} %bitcast.30) | data formatting | bytes 4194304 | tf_op jit(solution)/shard_map/transpose | solution.py:443
  67.4 0.0 copy-start.2
  67.4 3.5 %all-to-all-start.1 = ((f32[32,2,32,256]{3,2,1,0:T(8,128)}), f32[32,2,32,256]{3,2,1,0:T(8,128)S(1)}, u32[]{:S(2)}, u32[]{:S(2)}) async-start(f32[32,2,32,256]{3,2,1,0:T(8,128)} %bitcast.33), calls=%async_computation.1 | async-start | bytes 4194304 | tf_op jit(solution)/shard_map/all_to_all | solution.py:444
  70.9 0.0 copy-done.2
  70.9 0.2 slice.16
  71.1 0.2 slice.15
  71.4 0.6 pad_add_fusion
  71.9 0.6 fusion.5.order2_ref
  72.5 48.4 %all-to-all-done.1 = f32[32,2,32,256]{3,2,1,0:T(8,128)S(1)} async-done(((f32[32,2,32,256]{3,2,1,0:T(8,128)}), f32[32,2,32,256]{3,2,1,0:T(8,128)S(1)}, u32[]{:S(2)}, u32[]{:S(2)}) %all-to-all-start.1) | async-done | bytes 2097184 | tf_op jit(solution)/shard_map/all_to_all | solution.py:444
  120.9 0.0 copy-start
  120.9 1.3 copy-done
  122.3 52.7 %solve_modes.1 = (f32[64,32,256]{2,1,0:T(8,128)}, f32[2,32,128]{2,1,0:T(8,128)}) custom-call(s32[64]{0:T(128)} %outer_ref.1, f32[64,32,256]{2,1,0:T(8,128)} %bitcast.32, f32[32,1]{1,0:T(8,128)} %fusion.5.order2_ref, s32[1,256]{1,0:T(1,128)} %bitcast.41), custom_call_target="tpu_custom_call" | custom-call | tf_op jit(solution)/shard_map/solve_modes/pallas_call | solution.py:396
  174.9 2.7 all-to-all-start.2
  177.7 2.7 fusion.10
  180.4 1.3 copy.35
  181.7 3.0 %pad_maximum_fusion.table_ref = bf16[2,2,512,512]{3,2,1,0:T(8,128)(2,1)} fusion(bf16[1,2,512,512]{3,2,1,0:T(8,128)(2,1)} %get-tuple-element.7, bf16[1,2,512,512]{3,2,1,0:T(8,128)(2,1)} %copy.35), kind=kLoop, calls=%fused_computation | loop fusion | flops 1048576 | bytes 4194304 | tf_op jit(solution)/shard_map/stack | solution.py:434
  184.7 43.0 %all-to-all-done.2 = f32[32,2,32,256]{3,2,1,0:T(8,128)S(1)} async-done(((f32[32,2,32,256]{3,2,1,0:T(8,128)}), f32[32,2,32,256]{3,2,1,0:T(8,128)S(1)}, u32[]{:S(2)}, u32[]{:S(2)}) %all-to-all-start.2) | async-done | bytes 2097184 | tf_op jit(solution)/shard_map/all_to_all | solution.py:460
  227.7 1.6 copy.34
  229.3 5.4 %backward_transform.1 = f32[8,2,128,256]{3,2,1,0:T(8,128)} custom-call(f32[2,2,512,256]{3,2,1,0:T(8,128)} %bitcast.31, bf16[2,2,512,512]{3,2,1,0:T(8,128)(2,1)} %pad_maximum_fusion.table_ref, bf16[256,256]{1,0:T(8,128)(2,1)} %constant.55.clone.order_ref), custom_call_target="tpu_custom_call" | custom-call | tf_op jit(solution)/shard_map/backward_transform/pallas_call | solution.py:105
  234.7 0.0 copy-start.1
  234.7 3.7 %all-to-all-start.3 = ((f32[8,2,128,256]{3,2,1,0:T(8,128)}), f32[8,2,128,256]{3,2,1,0:T(8,128)S(1)}, u32[]{:S(2)}, u32[]{:S(2)}) async-start(f32[8,2,128,256]{3,2,1,0:T(8,128)} %backward_transform.1), calls=%async_computation.3 | async-start | bytes 4194304 | tf_op jit(solution)/shard_map/all_to_all | solution.py:464
  238.4 0.0 copy-done.1
  238.5 0.1 slice_reduce_fusion
  238.5 0.1 reshape_squeeze.3
  238.6 0.1 copy.37
  238.7 0.1 reshape.109
  238.8 7.1 %all-gather = f32[4,32,2]{1,2,0:T(2,128)S(1)} all-gather(f32[1,32,2]{1,2,0:T(2,128)S(1)} %bitcast.42), channel_id=1, replica_groups=mesh['phi'=8,'gz'=4] {'gz'}, dimensions={0}, use_global_device_ids=true | all-gather | bytes 1280 | tf_op jit(solution)/shard_map/all_gather | solution.py:457
  245.9 0.6 reshape.111
  246.6 40.8 %all-to-all-done.3 = f32[8,2,128,256]{3,2,1,0:T(8,128)S(1)} async-done(((f32[8,2,128,256]{3,2,1,0:T(8,128)}), f32[8,2,128,256]{3,2,1,0:T(8,128)S(1)}, u32[]{:S(2)}, u32[]{:S(2)}) %all-to-all-start.3) | async-done | bytes 2097184 | tf_op jit(solution)/shard_map/all_to_all | solution.py:464
  287.4 2.5 copy.40
  (1 shorter events, 0.0 us)
Async XLA Ops:
  67.4 3.5 %copy-start.2 = (s32[256]{0:T(256)S(1)}, s32[256]{0:T(256)}, u32[]{:S(2)}) copy-start(s32[256]{0:T(256)} %param.8) | copy-start | bytes 3076
  67.4 53.6 %all-to-all-start.1 = ((f32[32,2,32,256]{3,2,1,0:T(8,128)}), f32[32,2,32,256]{3,2,1,0:T(8,128)S(1)}, u32[]{:S(2)}, u32[]{:S(2)}) async-start(f32[32,2,32,256]{3,2,1,0:T(8,128)} %bitcast.33), calls=%async_computation.1 | async-start | bytes 4194304 | tf_op jit(solution)/shard_map/all_to_all | solution.py:444
  120.9 1.3 copy-start
  174.9 52.8 %all-to-all-start.2 = ((f32[32,2,32,256]{3,2,1,0:T(8,128)}), f32[32,2,32,256]{3,2,1,0:T(8,128)S(1)}, u32[]{:S(2)}, u32[]{:S(2)}) async-start(f32[32,2,32,256]{3,2,1,0:T(8,128)} %bitcast.38), calls=%async_computation.2 | async-start | bytes 4194304 | tf_op jit(solution)/shard_map/all_to_all | solution.py:460
  234.7 3.7 %copy-start.1 = (f32[2,32,128]{2,1,0:T(8,128)S(1)}, f32[2,32,128]{2,1,0:T(8,128)}, u32[]{:S(2)}) copy-start(f32[2,32,128]{2,1,0:T(8,128)} %get-tuple-element.5) | copy-start | bytes 98308
  234.7 52.7 %all-to-all-start.3 = ((f32[8,2,128,256]{3,2,1,0:T(8,128)}), f32[8,2,128,256]{3,2,1,0:T(8,128)S(1)}, u32[]{:S(2)}, u32[]{:S(2)}) async-start(f32[8,2,128,256]{3,2,1,0:T(8,128)} %backward_transform.1), calls=%async_computation.3 | async-start | bytes 4194304 | tf_op jit(solution)/shard_map/all_to_all | solution.py:464
